TPU v7x, 128 devices: a whole 4x4x4 slice. The times are simulated.
128 devices in a mesh: dp: 4 (over x_hi, core), fsdp: 8 (over z, x_lo), tensor: 4 (over y).
Axes of the slice: x: 4 (x_hi: 2, x_lo: 2; x = x_hi * 2 + x_lo), y: 4, z: 4, core: 2. Of those that a mesh axis runs over, the one named last changes fastest.
Arguments:
- tokens: bfloat16 [32, 768, 8192], P(('dp', 'fsdp'), 'tensor'), may hold values from -6 to 6
- norm_gain: float32 [8192], replicated, may hold values from 0.85 to 4
- w_qkv: bfloat16 [8192, 5120], P(('dp', 'fsdp'), 'tensor'), may hold values from -0.3 to 0.3
- a_query: bfloat16 [8192, 16], replicated, may hold values from -0.0625 to 0.0625
- query_up_adapter: bfloat16 [16, 4096], P(None, 'tensor'), may hold values from -1.5 to 1.5
- a_value: bfloat16 [8192, 16], replicated, may hold values from -0.0625 to 0.0625
- value_up_adapter: bfloat16 [16, 512], P(None, 'tensor'), may hold values from -1.5 to 1.5
- out_grad: bfloat16 [32, 768, 4096], P(('dp', 'fsdp'), 'tensor'), may hold values from -6 to 6
Outputs:
- attn_out: bfloat16 [32, 768, 4096], P(('dp', 'fsdp'), 'tensor')
- grad_a_query: float32 [8192, 16], replicated
- grad_b_query: float32 [16, 4096], P(None, 'tensor')
- grad_a_value: float32 [8192, 16], replicated
- grad_b_value: float32 [16, 512], P(None, 'tensor')
All inputs are finite; a program needn't handle non-finite values.
Results may differ from a plain program's by a relative error of at most 0.015.
The roundings to bfloat16 on the way count: a program that leaves them out, or rounds other values in their place, can miss the bound.
Values may be sent and summed in bfloat16 or wider, within the bound.
No kernel may reach another device: no remote copies, remote signals or barrier semaphores. Data moves between devices by JAX's collectives and lax.ppermute only.
A program may use at most 256 MiB of HBM per device.

v0:
```python
import math

import jax
import jax.numpy as jnp
from jax import lax
from jax.sharding import PartitionSpec as P

HD = 128
QUERY_PER_KV = 8


EPSILON = 1e-05
ADAPTER_SCALE = 2.0
ROPE_BASE = 500000.0


def from_everyone(array, axis):
    copies = jnp.broadcast_to(array, (lax.axis_size(axis), *array.shape))
    return lax.all_to_all(copies, axis, split_axis=0, concat_axis=0, tiled=True)


def joined_along(tiles, dim):
    lengths = list(tiles.shape[1:])
    lengths[dim] *= tiles.shape[0]
    return jnp.moveaxis(tiles, 0, dim).reshape(lengths)


def collect(array, axis, dim):
    tiles = from_everyone(array, axis)
    return joined_along(tiles, dim)


def of_everyone(array, axis):
    return from_everyone(array, axis).sum(axis=0)


def normalize(own_rows, norm_gain):
    widened = own_rows.astype(jnp.float32)
    mean_square = jnp.mean(widened * widened, axis=-1, keepdims=True)
    return (widened * lax.rsqrt(mean_square + EPSILON) * norm_gain).astype(jnp.bfloat16)


def rotary(heads_block):
    sequence_length = heads_block.shape[0]
    half_dim = heads_block.shape[-1] // 2
    positions = jnp.arange(sequence_length, dtype=jnp.float32)[:, None]
    inv_freq = ROPE_BASE ** (-jnp.arange(half_dim, dtype=jnp.float32) / half_dim)
    angles = positions * inv_freq
    cosine = jnp.cos(angles)[:, None, :]
    sine_table = jnp.sin(angles)[:, None, :]
    front_half = heads_block[..., :half_dim].astype(jnp.float32)
    back_half = heads_block[..., half_dim:].astype(jnp.float32)
    turned = jnp.concatenate(
        [
            front_half * cosine - back_half * sine_table,
            back_half * cosine + front_half * sine_table,
        ],
        -1,
    )
    return turned.astype(jnp.bfloat16)


def attend(query_rows, key_heads, value_rows):
    sequence_length = query_rows.shape[0]
    kv_heads = key_heads.shape[1] // HD
    rot_queries = rotary(query_rows.reshape(sequence_length, kv_heads * QUERY_PER_KV, HD))
    rot_keys = rotary(key_heads.reshape(sequence_length, kv_heads, HD))
    split_values = value_rows.reshape(sequence_length, kv_heads, HD)
    causal = jnp.arange(sequence_length)[:, None] >= jnp.arange(sequence_length)[None, :]

    def one_head(head_index):
        q_head = lax.dynamic_index_in_dim(rot_queries, head_index, 1, keepdims=False)
        k_head = lax.dynamic_index_in_dim(rot_keys, head_index // QUERY_PER_KV, 1, keepdims=False)
        v_head = lax.dynamic_index_in_dim(
            split_values, head_index // QUERY_PER_KV, 1, keepdims=False
        )
        scores = jnp.dot(q_head, k_head.T, preferred_element_type=jnp.float32) * (
            1.0 / math.sqrt(HD)
        )
        scores = jnp.where(causal, scores, -1e30)
        row_max = jnp.max(scores, axis=-1, keepdims=True)
        weights = jnp.exp(scores - row_max)
        probabilities = (weights / jnp.sum(weights, axis=-1, keepdims=True)).astype(jnp.bfloat16)
        return jnp.dot(probabilities, v_head, preferred_element_type=jnp.float32).astype(
            jnp.bfloat16
        )

    per_head = lax.map(one_head, jnp.arange(kv_heads * QUERY_PER_KV, dtype=jnp.int32))
    return jnp.transpose(per_head, (1, 0, 2)).reshape(sequence_length, kv_heads * QUERY_PER_KV * HD)


def local(tokens, norm_gain, w_qkv, a_query, query_up_adapter, a_value, value_up_adapter, out_grad):
    normed_input = normalize(tokens[0], norm_gain)
    gathered = collect(normed_input, "tensor", 0)
    sequence_length = gathered.shape[0]
    col_count = w_qkv.shape[1]
    weights = lax.all_gather(w_qkv, ("dp", "fsdp"), axis=0, tiled=True)
    projected = jnp.dot(gathered, weights, preferred_element_type=jnp.float32)
    narrow_rank_rows = a_query.shape[1]
    down_projected = jnp.dot(
        gathered, jnp.concatenate([a_query, a_value], 1), preferred_element_type=jnp.float32
    ).astype(jnp.bfloat16)
    kv_local = col_count // ((QUERY_PER_KV + 2) * HD)
    grouped_queries = projected.reshape(sequence_length, kv_local, QUERY_PER_KV + 2, HD)
    query_rows = (
        grouped_queries[:, :, :QUERY_PER_KV].reshape(sequence_length, -1)
        + ADAPTER_SCALE
        * jnp.dot(
            down_projected[:, :narrow_rank_rows],
            query_up_adapter,
            preferred_element_type=jnp.float32,
        )
    ).astype(jnp.bfloat16)
    key_heads = (
        grouped_queries[:, :, QUERY_PER_KV].reshape(sequence_length, -1).astype(jnp.bfloat16)
    )
    value_rows = (
        grouped_queries[:, :, QUERY_PER_KV + 1].reshape(sequence_length, -1)
        + ADAPTER_SCALE
        * jnp.dot(
            down_projected[:, narrow_rank_rows:],
            value_up_adapter,
            preferred_element_type=jnp.float32,
        )
    ).astype(jnp.bfloat16)
    grad_rows = lax.all_to_all(out_grad[0], "tensor", split_axis=1, concat_axis=0, tiled=True)
    attended, pullback = jax.vjp(attend, query_rows, key_heads, value_rows)
    query_gradient, grad_keys, value_gradient = pullback(grad_rows)
    out_rows = lax.all_to_all(attended, "tensor", split_axis=0, concat_axis=1, tiled=True)
    query_up_gradient = ADAPTER_SCALE * jnp.einsum(
        "fb,fd->bd",
        down_projected[:, :narrow_rank_rows],
        query_gradient,
        preferred_element_type=jnp.float32,
    )
    value_up_gradient = ADAPTER_SCALE * jnp.einsum(
        "fb,fd->bd",
        down_projected[:, narrow_rank_rows:],
        value_gradient,
        preferred_element_type=jnp.float32,
    )
    middle_gradient = jnp.concatenate(
        [
            jnp.dot(query_gradient, query_up_adapter.T, preferred_element_type=jnp.float32),
            jnp.dot(value_gradient, value_up_adapter.T, preferred_element_type=jnp.float32),
        ],
        1,
    )
    mid_summed = of_everyone(middle_gradient, "tensor").astype(jnp.bfloat16)
    down_gradient = ADAPTER_SCALE * jnp.einsum(
        "uh,ux->hx", gathered, mid_summed, preferred_element_type=jnp.float32
    )
    down_gradient, query_up_gradient, value_up_gradient = lax.psum(
        (down_gradient, query_up_gradient, value_up_gradient), ("dp", "fsdp")
    )
    return (
        out_rows[None],
        down_gradient[:, :narrow_rank_rows],
        query_up_gradient,
        down_gradient[:, narrow_rank_rows:],
        value_up_gradient,
    )


def solution(mesh):
    return jax.shard_map(
        local,
        mesh=mesh,
        in_specs=(
            P(("dp", "fsdp"), "tensor", None),
            P(),
            P(("dp", "fsdp"), "tensor"),
            P(),
            P(None, "tensor"),
            P(),
            P(None, "tensor"),
            P(("dp", "fsdp"), "tensor", None),
        ),
        out_specs=(
            P(("dp", "fsdp"), "tensor", None),
            P(),
            P(None, "tensor"),
            P(),
            P(None, "tensor"),
        ),
        check_vma=False,
    )
```

profile of v0, /device:TPU:0, one launch (start us, length us, event | category | flops | bytes accessed | tf_op | source)
XLA Modules:
  0.0 583.8 jit_solution(4451052558381677844)
XLA Ops:
  7.9 3.9 all_to_all.34
  11.8 3.2 copy.69
  15.0 4.6 all-to-all-start.2
  22.8 17.7 %all-to-all-done.2 = bf16[192,4,1024]{2,0,1:T(8,128)(2,1)} async-done(((bf16[192,4,1024]{2,0,1:T(8,128)(2,1)}), bf16[192,4,1024]{2,0,1:T(8,128)(2,1)}, u32[]{:S(2)}, u32[]{:S(2)}) %all-to-all-start.2) | async-done | bytes 1572896 | tf_op jit(solution)/shard_map/all_to_all | solution.py:126
  40.4 8.0 %broadcast_in_dim.206 = bf16[4,192,8192]{2,1,0:T(8,128)(2,1)} broadcast(bf16[192,8192]{1,0:T(8,128)(2,1)} %fusion.64), dimensions={1,2} | broadcast | bytes 15728640 | tf_op jit(solution)/shard_map/broadcast_in_dim | solution.py:18
  48.4 6.6 %all-to-all-start = ((bf16[4,192,8192]{2,1,0:T(8,128)(2,1)}), bf16[4,192,8192]{2,1,0:T(8,128)(2,1)}, u32[]{:S(2)}, u32[]{:S(2)}) async-start(bf16[4,192,8192]{2,1,0:T(8,128)(2,1)} %broadcast_in_dim.206), calls=%async_computation | async-start | bytes 25165824 | tf_op jit(solution)/shard_map/all_to_all | solution.py:19
  60.0 132.8 %all-to-all-done = bf16[4,192,8192]{2,1,0:T(8,128)(2,1)} async-done(((bf16[4,192,8192]{2,1,0:T(8,128)(2,1)}), bf16[4,192,8192]{2,1,0:T(8,128)(2,1)}, u32[]{:S(2)}, u32[]{:S(2)}) %all-to-all-start) | async-done | bytes 12582944 | tf_op jit(solution)/shard_map/all_to_all | solution.py:19
  192.9 8.4 %convolution_convert_fusion.2 = bf16[768,32]{0,1:T(8,128)(2,1)S(1)} fusion(bf16[768,8192]{1,0:T(8,128)(2,1)} %bitcast.2, bf16[8192,16]{0,1:T(8,128)(2,1)S(1)} %copy-done.8, bf16[8192,16]{0,1:T(8,128)(2,1)S(1)} %copy-done.9), kind=kOutput, calls=%fused_computation.95 | convolution fusion | flops 403726336 | bytes 13156352 | tf_op jit(solution)/shard_map/dot_general | solution.py:100
  201.3 27.0 %copy.60 = bf16[1280,8192]{1,0:T(8,128)(2,1)} copy(bf16[1280,8192]{0,1:T(8,128)(2,1)} %bitcast.185) | data formatting | bytes 41943040 | tf_op jit(solution)/shard_map/dot_general | solution.py:98
  228.3 21.0 %convolution_bitcast_fusion = f32[768,1,10,128]{0,3,2,1:T(8,128)S(1)} fusion(bf16[768,8192,1]{1,0,2:T(8,128)(2,1)} %bitcast.3, bf16[10,128,8192]{2,1,0:T(8,128)(2,1)} %bitcast.186), kind=kOutput, calls=%fused_computation.78 | convolution fusion | flops 16106127360 | bytes 37486592 | tf_op jit(solution)/shard_map/dot_general | solution.py:98
  261.6 87.0 %while.52 = (s32[]{:T(128)}, bf16[8,768,128]{2,1,0:T(8,128)(2,1)}, s32[8]{0:T(128)S(1)}, bf16[8,128,768]{2,1,0:T(8,128)(2,1)}, f32[8,768,768]{1,2,0:T(8,128)}, /...) while((s32[]{:T(128)}, bf16[8,768,128]{2,1,0:T(8,128)(2,1)}, ...), condition=%wide.region_5.6_spmd.clone, body=%wide.region_1.5_spmd.clone.sunk | while | flops 310344960 | bytes 20494060 | solution.py:88
  348.8 93.7 %while.53 = (s32[]{:T(128)}, bf16[768,8,128]{0,2,1:T(8,128)(2,1)S(1)}, bf16[768,1,128]{2,0,1:T(8,128)(2,1)S(1)}, s32[8]{0:T(128)S(1)}, bf16[8,768,128]{2,1,0:T(8...) while((s32[]{:T(128)}, ...), condition=%wide.region_9.10_spmd.clone, body=%wide.region_6.9_spmd.clone.sunk | while | flops 464683776 | bytes 17364168 | solution.py:88
  354.8 3.0 fusion.132
  366.5 3.0 fusion.132
  389.9 3.0 fusion.132
  401.7 3.0 fusion.132
  425.1 3.0 fusion.132
  436.8 3.0 fusion.132
  445.4 3.5 all-to-all-start.3
  450.1 6.1 %all-to-all-done.3 = f32[4,768,32]{1,2,0:T(8,128)S(1)} async-done(((f32[4,768,32]{1,2,0:T(8,128)}), f32[4,768,32]{1,2,0:T(8,128)S(1)}, u32[]{:S(2)}, u32[]{:S(2)}) %all-to-all-start.3) | async-done | bytes 393248 | tf_op jit(solution)/shard_map/all_to_all | solution.py:19
  456.3 7.9 %convolution_multiply_fusion = f32[8192,32]{0,1:T(8,128)} fusion(bf16[768,8192]{1,0:T(8,128)(2,1)} %bitcast.2, bf16[768,32]{0,1:T(8,128)(2,1)S(1)} %reduce_sum.89), kind=kOutput, calls=%fused_computation.71 | convolution fusion | flops 402915328 | bytes 13680640 | tf_op jit(solution)/shard_map/uh,ux->hx/dot_general | solution.py:150
  467.3 3.6 all-to-all-start.1
  471.0 67.1 %psum.23 = f32[16,128]{1,0:T(8,128)} all-reduce(f32[16,128]{1,0:T(8,128)S(1)} %convolution_multiply_fusion.3), channel_id=1, replica_groups=mesh['dp'=4,'fsdp'=8,'tensor'=4] {'dp','fsdp'}, use_global_device_ids=true, to_apply=%region_13.14 | all-reduce | flops 2048 | bytes 16384 | tf_op jit(solution)/shard_map/psum | solution.py:153
  538.1 32.3 %all-reduce.5.cloned.1.call-done = (f32[8192,32]{0,1:T(8,128)}, f32[16,1024]{1,0:T(8,128)}) async-done(((f32[8192,32]{0,1:T(8,128)}, f32[16,1024]{1,0:T(8,128)}), (f32[8192,32]{0,1:T(8,128)}, f32[16,1024]{1,0:T(8,128)})) %all-reduce.5.cloned.1.call-update) | async-done | bytes 1114128 | tf_op jit(solution)/shard_map/psum | solution.py:153
  (273 shorter events, 180.2 us)
Async XLA Ops:
  7.2 247.1 %copy-start = (bf16[16,1024]{1,0:T(8,128)(2,1)S(1)}, bf16[16,1024]{1,0:T(8,128)(2,1)}, u32[]{:S(2)}) copy-start(bf16[16,1024]{1,0:T(8,128)(2,1)} %param.16) | copy-start | bytes 98308
  7.2 194.1 %all-gather.2.cloned.1.call-start = ((), (), s32[]{:S(2)}) async-start(), calls=%async_computation.4 | async-start | bytes 21626880 | tf_op jit(solution)/shard_map/all_gather | solution.py:97
  11.8 7.8 %copy-start.1 = (bf16[1,192,8192]{2,1,0:T(8,128)(2,1)S(1)}, bf16[1,192,8192]{2,1,0:T(8,128)(2,1)}, u32[]{:S(2)}) copy-start(bf16[1,192,8192]{2,1,0:T(8,128)(2,1)} %param.12) | copy-start | bytes 9437188
  15.0 25.5 %all-to-all-start.2 = ((bf16[192,4,1024]{2,0,1:T(8,128)(2,1)}), bf16[192,4,1024]{2,0,1:T(8,128)(2,1)}, u32[]{:S(2)}, u32[]{:S(2)}) async-start(bf16[192,4,1024]{2,0,1:T(8,128)(2,1)} %copy.69), calls=%async_computation.2 | async-start | bytes 3145728 | tf_op jit(solution)/shard_map/all_to_all | solution.py:126
  19.6 0.8 copy-start.11
  48.4 144.4 %all-to-all-start = ((bf16[4,192,8192]{2,1,0:T(8,128)(2,1)}), bf16[4,192,8192]{2,1,0:T(8,128)(2,1)}, u32[]{:S(2)}, u32[]{:S(2)}) async-start(bf16[4,192,8192]{2,1,0:T(8,128)(2,1)} %broadcast_in_dim.206), calls=%async_computation | async-start | bytes 25165824 | tf_op jit(solution)/shard_map/all_to_all | solution.py:19
  58.6 134.3 %copy-start.8 = (bf16[8192,16]{0,1:T(8,128)(2,1)S(1)}, bf16[8192,16]{0,1:T(8,128)(2,1)}, u32[]{:S(2)}) copy-start(bf16[8192,16]{0,1:T(8,128)(2,1)} %param.17) | copy-start | bytes 786436
  58.6 134.2 %copy-start.9 = (bf16[8192,16]{0,1:T(8,128)(2,1)S(1)}, bf16[8192,16]{0,1:T(8,128)(2,1)}, u32[]{:S(2)}) copy-start(bf16[8192,16]{0,1:T(8,128)(2,1)} %param.15) | copy-start | bytes 786436
  249.3 1.9 copy-start.2
  256.8 0.9 copy-start.7
  256.8 1.8 copy-start.12
  261.6 87.2 %copy-start.6 = (bf16[768,1,128]{2,0,1:T(8,128)(2,1)S(1)}, bf16[768,1,128]{2,0,1:T(8,128)(2,1)}, u32[]{:S(2)}) copy-start(bf16[768,1,128]{2,0,1:T(8,128)(2,1)} %custom-call) | copy-start | bytes 589828
  442.5 0.9 copy-start.3
  442.5 1.0 copy-start.4
  445.4 10.8 %all-to-all-start.3 = ((f32[4,768,32]{1,2,0:T(8,128)}), f32[4,768,32]{1,2,0:T(8,128)S(1)}, u32[]{:S(2)}, u32[]{:S(2)}) async-start(f32[4,768,32]{1,2,0:T(8,128)} %broadcast_in_dim.210), calls=%async_computation.3 | async-start | bytes 786432 | tf_op jit(solution)/shard_map/all_to_all | solution.py:19
  448.9 121.6 %all-reduce.5.cloned.1.call-start = ((), (), s32[]{:S(2)}) async-start(), calls=%async_computation.5 | async-start | bytes 2228224 | tf_op jit(solution)/shard_map/psum | solution.py:153
  456.3 8.0 %copy-start.5 = (bf16[8,768,128]{2,1,0:T(8,128)(2,1)S(1)}, bf16[8,768,128]{2,1,0:T(8,128)(2,1)}, u32[]{:S(2)}) copy-start(bf16[8,768,128]{2,1,0:T(8,128)(2,1)} %get-tuple-element.648) | copy-start | bytes 4718596
  467.3 105.4 %all-to-all-start.1 = ((bf16[4,192,1024]{2,1,0:T(8,128)(2,1)}), bf16[4,192,1024]{2,1,0:T(8,128)(2,1)S(1)}, u32[]{:S(2)}, u32[]{:S(2)}) async-start(bf16[4,192,1024]{2,1,0:T(8,128)(2,1)} %all_to_all.31), calls=%async_computation.1 | async-start | bytes 3145728 | tf_op jit(solution)/shard_map/all_to_all | solution.py:129
  573.9 2.4 copy-start.10
Sparse Core Ops, SparseCore 0:
  9.7 123.8 all-gather.1
  464.4 106.0 all-reduce.4
where the time goes:
time: 587 us; the launch traced here: 584 us
  waiting for transfers between devices  190 us (32%)
  matrix products  115 us (20%)
  local copies, waits for them, and re-layouts  98.5 us (17%)
  blocking collectives  67.1 us (11%)
  other arithmetic  63.1 us (11%)
  starting transfers between devices  18.3 us (3%)
  loops' own time  17.5 us (3%)
  between operations  14.4 us (2%)
    all_to_all x2, waiting for transfers between devices, from_everyone(): return lax.all_to_all(copies, axis, split_axis=0, concat_axis=0, tiled=True)  139 us
    psum x1, blocking collectives, local(): lax.psum((down_gradient, query_up_gradient, value_up_gradient), ('dp', 'f...  67.1 us
    dot_general x24, matrix products, one_head(): jnp.dot(probabilities, v_head, preferred_element_type=jnp.float32)  43.6 us
    psum x1, waiting for transfers between devices, local(): lax.psum((down_gradient, query_up_gradient, value_up_gradient), ('dp', 'f...  32.3 us
    dynamic_update_slice x24, other arithmetic, attend(): lax.map(one_head, jnp.arange(kv_heads * QUERY_PER_KV, dtype=jnp.int32))  31.9 us
    dot_general x16, matrix products, one_head(): jnp.dot(q_head, k_head.T, preferred_element_type=jnp.float32)  28.8 us
    dot_general x1, local copies, waits for them, and re-layouts, local(): projected = jnp.dot(gathered, weights, preferred_element_type=jnp.float32)  27 us
    dot_general x1, matrix products, local(): projected = jnp.dot(gathered, weights, preferred_element_type=jnp.float32)  21 us
  transfers between devices with their start and end apart: 6, of which 4 were waited for; matrix products, arithmetic and copies ran while one was open for 6% of the time, Pallas kernels for 0%

commit v1 on v0

v1 whole, which is shorter than its diff:
```python
import functools
import math

import jax
import jax.numpy as jnp
from jax import lax
from jax.experimental import pallas as pl
from jax.experimental.pallas import tpu as pltpu
from jax.sharding import PartitionSpec as P

HD = 128
QUERY_PER_KV = 8


EPSILON = 1e-05
ADAPTER_SCALE = 2.0
ROPE_BASE = 500000.0
WHERE = ("dp", "fsdp")
NT = (((1,), (1,)), ((), ()))
TN = (((0,), (0,)), ((), ()))


def ring(size, step):
    return [(i, (i + step) % size) for i in range(size)]


def normalize(own_rows, norm_gain):
    widened = own_rows.astype(jnp.float32)
    mean_square = jnp.mean(widened * widened, axis=-1, keepdims=True)
    return (widened * lax.rsqrt(mean_square + EPSILON) * norm_gain).astype(jnp.bfloat16)


def rotary_tables(sequence_length):
    half_dim = HD // 2
    positions = jnp.arange(sequence_length, dtype=jnp.float32)[:, None]
    inv_freq = ROPE_BASE ** (-jnp.arange(half_dim, dtype=jnp.float32) / half_dim)
    angles = positions * inv_freq
    cosine = jnp.cos(angles)
    sine = jnp.sin(angles)
    return jnp.concatenate([cosine, cosine], 1), jnp.concatenate([-sine, sine], 1)


def attention_kernel(
    block, q_ref, k_ref, v_ref, down_ref, up_q_ref, up_v_ref, grad_ref, cos_ref, sin_ref,
    out_ref, grad_b_q_ref, grad_b_v_ref, mid_ref,
    keys, keys_t, values, values_t, grad_values_t, mid_q,
):
    head = pl.program_id(0)
    last = pl.num_programs(0) - 1
    length = q_ref.shape[0]
    rank = up_q_ref.shape[0]
    f32, bf16 = jnp.float32, jnp.bfloat16
    dot = functools.partial(jnp.dot, preferred_element_type=f32)
    dot_general = functools.partial(lax.dot_general, preferred_element_type=f32)
    scale = 1.0 / math.sqrt(HD)
    to_exp2 = scale * math.log2(math.e)

    def turned(x, cosine, sine):
        return x * cosine + pltpu.roll(x, HD // 2, 1) * sine

    @pl.when(head == 0)
    def _():
        k = turned(k_ref[...].astype(bf16).astype(f32), cos_ref[...], sin_ref[...])
        keys[...] = k.astype(bf16)
        keys_t[...] = k.T.astype(bf16)
        v = v_ref[...] + ADAPTER_SCALE * dot(down_ref[:, rank:], up_v_ref[...])
        values[...] = v.astype(bf16)
        values_t[...] = v.T.astype(bf16)
        grad_values_t[...] = jnp.zeros_like(grad_values_t)
        mid_q[...] = jnp.zeros_like(mid_q)

    up_q = up_q_ref[...]
    grad_b = jnp.zeros(grad_b_q_ref.shape, f32)
    for index in range(length // block):
        rows = pl.ds(index * block, block)
        seen = (index + 1) * block
        down = down_ref[rows, :rank]
        cosine, sine = cos_ref[rows, :], sin_ref[rows, :]
        q = (q_ref[rows, :] + ADAPTER_SCALE * dot(down, up_q)).astype(bf16)
        q = turned(q.astype(f32), cosine, sine).astype(bf16)
        scores = dot(q, keys_t[:, :seen])
        row_ids = lax.broadcasted_iota(jnp.int32, (block, block), 0)
        col_ids = lax.broadcasted_iota(jnp.int32, (block, block), 1)
        diagonal = jnp.where(row_ids >= col_ids, scores[:, seen - block :], -1e30)
        if index:
            scores = jnp.concatenate([scores[:, : seen - block], diagonal], 1)
        else:
            scores = diagonal
        scores = scores * to_exp2
        weights = jnp.exp2(scores - jnp.max(scores, axis=-1, keepdims=True))
        probabilities = weights * (1.0 / jnp.sum(weights, axis=-1, keepdims=True))
        rounded = probabilities.astype(bf16)
        attended = dot(rounded, values[:seen, :])
        out_ref[rows, :] = attended.astype(bf16)
        grad_out = grad_ref[rows, :]
        grad_f32 = grad_out.astype(f32)
        grad_p = dot(grad_out, values_t[:, :seen])
        along = jnp.sum(grad_f32 * attended, axis=-1, keepdims=True)
        grad_scores = (probabilities * (grad_p - along)).astype(bf16)
        grad_q = (dot(grad_scores, keys[:seen, :]) * scale).astype(bf16).astype(f32)
        grad_q = turned(grad_q, cosine, -sine).astype(bf16)
        grad_values_t[:, :seen] += dot(grad_f32.T.astype(bf16), rounded)
        grad_b += dot_general(down, grad_q, TN)
        mid_q[rows, :] += dot_general(grad_q, up_q, NT)
    grad_b_q_ref[...] = ADAPTER_SCALE * grad_b

    @pl.when(head == last)
    def _():
        grad_v = grad_values_t[...].T.astype(bf16)
        grad_b_v_ref[...] = ADAPTER_SCALE * dot_general(down_ref[:, rank:], grad_v, TN)
        mid_ref[:, :rank] = mid_q[...]
        mid_ref[:, rank:] = dot_general(grad_v, up_v_ref[...], NT)


def attention(projected, down, up_q, up_v, grad_rows, cosine, sine):
    length = projected.shape[0]
    rank = up_q.shape[0]
    heads = up_q.shape[1] // HD
    block = 256
    whole = lambda h: (0, 0)
    column = lambda h: (0, h)
    f32, bf16 = jnp.float32, jnp.bfloat16
    return pl.pallas_call(
        functools.partial(attention_kernel, block),
        grid=(heads,),
        in_specs=[
            pl.BlockSpec((length, HD), column),
            pl.BlockSpec((length, HD), lambda h: (0, heads)),
            pl.BlockSpec((length, HD), lambda h: (0, heads + 1)),
            pl.BlockSpec((length, 2 * rank), whole),
            pl.BlockSpec((rank, HD), column),
            pl.BlockSpec((rank, HD), whole),
            pl.BlockSpec((length, HD), column),
            pl.BlockSpec((length, HD), whole),
            pl.BlockSpec((length, HD), whole),
        ],
        out_specs=[
            pl.BlockSpec((length, HD), column),
            pl.BlockSpec((rank, HD), column),
            pl.BlockSpec((rank, HD), whole),
            pl.BlockSpec((length, 2 * rank), whole),
        ],
        out_shape=[
            jax.ShapeDtypeStruct((length, heads * HD), bf16),
            jax.ShapeDtypeStruct((rank, heads * HD), f32),
            jax.ShapeDtypeStruct((rank, HD), f32),
            jax.ShapeDtypeStruct((length, 2 * rank), f32),
        ],
        scratch_shapes=[
            pltpu.VMEM((length, HD), bf16),
            pltpu.VMEM((HD, length), bf16),
            pltpu.VMEM((length, HD), bf16),
            pltpu.VMEM((HD, length), bf16),
            pltpu.VMEM((HD, length), f32),
            pltpu.VMEM((length, rank), f32),
        ],
        compiler_params=pltpu.CompilerParams(dimension_semantics=("arbitrary",)),
        name="attention",
    )(projected, projected, projected, down, up_q, up_v, grad_rows, cosine, sine)


def local(tokens, norm_gain, w_qkv, a_query, query_up_adapter, a_value, value_up_adapter, out_grad):
    f32, bf16 = jnp.float32, jnp.bfloat16
    size = lax.axis_size("tensor")
    me = lax.axis_index("tensor")
    rank = a_query.shape[1]
    own = out_grad.shape[1]
    length = own * size
    q_cols = query_up_adapter.shape[1]

    weights = lax.all_gather(w_qkv, WHERE, axis=0, tiled=True)
    grad_rows = lax.all_to_all(out_grad[0], "tensor", split_axis=1, concat_axis=0, tiled=True)

    normed = normalize(tokens[0], norm_gain)
    ahead, behind = ring(size, 1), ring(size, -1)
    from_left = lax.ppermute(normed, "tensor", ahead)
    from_right = lax.ppermute(normed, "tensor", behind)
    half = own // 2
    far_top = lax.ppermute(from_left[:half], "tensor", ahead)
    far_low = lax.ppermute(from_right[half:], "tensor", behind)
    gathered = jnp.zeros((length, normed.shape[1]), bf16)
    for rows, place in (
        (normed, me * own),
        (from_left, (me + size - 1) % size * own),
        (from_right, (me + 1) % size * own),
        (far_top, (me + 2) % size * own),
        (far_low, (me + 2) % size * own + half),
    ):
        gathered = lax.dynamic_update_slice(gathered, rows, (place, 0))

    adapters = jnp.concatenate([a_query, a_value], 1)
    down = jnp.dot(gathered, adapters, preferred_element_type=f32).astype(bf16)
    projected = jnp.dot(gathered, weights, preferred_element_type=f32)
    cosine, sine = rotary_tables(length)
    attended, grad_b_q, grad_b_v, mid = attention(
        projected, down, query_up_adapter, value_up_adapter, grad_rows, cosine, sine
    )
    out_rows = lax.all_to_all(attended, "tensor", split_axis=0, concat_axis=1, tiled=True)

    spread = jnp.broadcast_to(mid[None], (size, *mid.shape))
    mid_sum = lax.all_to_all(spread, "tensor", 0, 0, tiled=True).sum(axis=0).astype(bf16)
    part = normed.shape[1] // size
    features = lax.dynamic_slice(gathered, (0, me * part), (length, part))
    grad_a = ADAPTER_SCALE * lax.dot_general(mid_sum, features, TN, preferred_element_type=f32)

    groups = lax.axis_size(WHERE)
    packed = jnp.concatenate(
        [
            grad_a.reshape(groups, -1),
            grad_b_q.reshape(groups, -1),
            grad_b_v.reshape(groups, -1),
        ],
        1,
    )
    width = packed.shape[1]
    padded = -(-width // 1024) * 1024
    packed = jnp.pad(packed, ((0, 0), (0, padded - width))).reshape(groups, 8, padded // 8)
    summed = lax.all_to_all(packed, WHERE, 0, 0, tiled=True).sum(axis=0)
    shared = lax.all_gather(summed, WHERE, axis=0, tiled=False).reshape(groups, padded)
    n_a, n_q, n_v = grad_a.size // groups, grad_b_q.size // groups, grad_b_v.size // groups
    grad_a = shared[:, :n_a].reshape(grad_a.shape)
    grad_b_q = shared[:, n_a : n_a + n_q].reshape(grad_b_q.shape)
    grad_b_v = shared[:, n_a + n_q : n_a + n_q + n_v].reshape(grad_b_v.shape)
    grad_a = lax.all_gather(grad_a, "tensor", axis=1, tiled=True)
    return out_rows[None], grad_a[:rank].T, grad_b_q, grad_a[rank:].T, grad_b_v


def solution(mesh):
    return jax.shard_map(
        local,
        mesh=mesh,
        in_specs=(
            P(("dp", "fsdp"), "tensor", None),
            P(),
            P(("dp", "fsdp"), "tensor"),
            P(),
            P(None, "tensor"),
            P(),
            P(None, "tensor"),
            P(("dp", "fsdp"), "tensor", None),
        ),
        out_specs=(
            P(("dp", "fsdp"), "tensor", None),
            P(),
            P(None, "tensor"),
            P(),
            P(None, "tensor"),
        ),
        check_vma=False,
    )
```

time: 587 us -> 344 us (0.59)
  matrix products: 115 us -> 33.3 us
  waiting for transfers between devices: 190 us -> 121 us
  local copies, waits for them, and re-layouts: 98.5 us -> 35.5 us
  other arithmetic: 63.1 us -> 9.19 us
  Pallas kernels: 0 us -> 29.8 us
  loops' own time: 17.5 us -> 0 us
  blocking collectives: 67.1 us -> 82.6 us
    all_to_all x2 -> x1, waiting for transfers between devices: 139 us -> 5.89 us  [local(): lax.all_to_all(spread, 'tensor', 0, 0, tiled=True).sum(axis=0).astype(bf16)]
    ppermute x0 -> x4, waiting for transfers between devices: none -> 93.5 us  [the longest x1 55.1 us: local(): from_left = lax.ppermute(normed, 'tensor', ahead)]
    dot_general x49 -> x3, matrix products: 115 us -> 33.3 us  [the longest x1 22.3 us: local(): projected = jnp.dot(gathered, weights, preferred_element_type=f32)]
    psum x1 -> x0, blocking collectives: 67.1 us -> none  [local(): lax.psum((down_gradient, query_up_gradient, value_up_gradient), ('dp', 'f...]
    all_gather x0 -> x1, blocking collectives: none -> 64.8 us  [local(): lax.all_gather(summed, WHERE, axis=0, tiled=False).reshape(groups, padded)]
    psum x1 -> x0, waiting for transfers between devices: 32.3 us -> none  [local(): lax.psum((down_gradient, query_up_gradient, value_up_gradient), ('dp', 'f...]
    pallas_call x0 -> x1, Pallas kernels: none -> 29.8 us  [attention(): pl.pallas_call(functools.partial(attention_kernel, block), grid=(heads,),...]
    dynamic_update_slice x24 -> x1, other arithmetic: 31.9 us -> 3.83 us  [local(): gathered = lax.dynamic_update_slice(gathered, rows, (place, 0))]
  transfers between devices with their start and end apart: 6 -> 9, of which waited for: 4 -> 4; matrix products, arithmetic and copies ran while one was open for 6% -> 19% of each run, Pallas kernels for 0% -> 0%
where the time goes in v1:
time: 344 us
  waiting for transfers between devices  121 us (35%)
  blocking collectives  82.6 us (24%)
  local copies, waits for them, and re-layouts  35.5 us (10%)
  matrix products  33.3 us (10%)
  Pallas kernels  29.8 us (9%)
  starting transfers between devices  18.3 us (5%)
  between operations  14.2 us (4%)
  other arithmetic  9.19 us (3%)
    all_gather x1, blocking collectives, local(): lax.all_gather(summed, WHERE, axis=0, tiled=False).reshape(groups, padded)  64.8 us
    ppermute x1, waiting for transfers between devices, local(): from_left = lax.ppermute(normed, 'tensor', ahead)  55.1 us
    ppermute x1, waiting for transfers between devices, local(): far_top = lax.ppermute(from_left[:half], 'tensor', ahead)  38.4 us
    pallas_call x1, Pallas kernels, attention(): pl.pallas_call(functools.partial(attention_kernel, block), grid=(heads,),...  29.8 us
    dot_general x1, matrix products, local(): projected = jnp.dot(gathered, weights, preferred_element_type=f32)  22.3 us
    all_to_all x1, waiting for transfers between devices, local(): lax.all_to_all(attended, 'tensor', split_axis=0, concat_axis=1, tiled=True)  20.6 us
    all_to_all x1, blocking collectives, local(): summed = lax.all_to_all(packed, WHERE, 0, 0, tiled=True).sum(axis=0)  17.9 us
    dynamic_update_slice x4, local copies, waits for them, and re-layouts, local(): gathered = lax.dynamic_update_slice(gathered, rows, (place, 0))  8.46 us
  transfers between devices with their start and end apart: 9, of which 4 were waited for; matrix products, arithmetic and copies ran while one was open for 19% of the time, Pallas kernels for 0%

profile of v1, /device:TPU:0, one launch (start us, length us, event | category | flops | bytes accessed | tf_op | source)
XLA Modules:
  0.0 343.6 jit_solution(17771145071703690958)
XLA Ops:
  7.9 2.6 fusion
  10.5 6.0 %broadcast_in_dim.6 = bf16[768,8192]{1,0:T(8,128)(2,1)} broadcast(bf16[]{:T(256)} %constant.44.clone.1), dimensions={} | broadcast | bytes 12582914 | tf_op jit(solution)/shard_map/broadcast_in_dim | solution.py:181
  16.6 3.8 %constant_dynamic-update-slice_fusion.4 = (bf16[768,8192]{1,0:T(8,128)(2,1)}, bf16[192,8192]{1,0:T(8,128)(2,1)}) fusion(bf16[768,8192]{1,0:T(8,128)(2,1)} %broadcast_in_dim.6, s32[]{:T(128)S(6)} %select_n.35, f32[8192]{0:T(1024)S(1)} %copy-done.3, f32[192]{0:T(256)S(1)} %add_rsqrt_fusion, bf16[1,192,8192]{2,1,0:T(8,128)(2,1)S(1)} %copy-done), kind=kLoop, calls=%fused_computation.29 | loop fusion | flops 6291456 | bytes 9470724 | tf_op jit(solution)/shard_map/dynamic_update_slice | solution.py:189
  20.4 1.6 collective-permute-start
  23.7 3.9 %all_to_all.32 = bf16[192,4,1024]{2,1,0:T(4,128)(2,1)} reshape(bf16[1,192,4096]{2,1,0:T(8,128)(2,1)} %param.15) | data formatting | bytes 3145728 | tf_op jit(solution)/shard_map/all_to_all | solution.py:172
  27.5 3.1 copy.24
  30.6 4.4 %all-to-all-start = ((bf16[192,4,1024]{2,0,1:T(8,128)(2,1)}), bf16[192,4,1024]{2,0,1:T(8,128)(2,1)}, u32[]{:S(2)}, u32[]{:S(2)}) async-start(bf16[192,4,1024]{2,0,1:T(8,128)(2,1)} %copy.24), calls=%async_computation | async-start | bytes 3145728 | tf_op jit(solution)/shard_map/all_to_all | solution.py:172
  37.7 55.1 %collective-permute-done = bf16[192,8192]{1,0:T(8,128)(2,1)S(1)} collective-permute-done((bf16[192,8192]{1,0:T(8,128)(2,1)}, bf16[192,8192]{1,0:T(8,128)(2,1)S(1)}, u32[]{:S(2)}, u32[]{:S(2)}) %collective-permute-start) | collective-permute-done | bytes 3145760 | tf_op jit(solution)/shard_map/ppermute | solution.py:176
  95.0 3.1 collective-permute-start.3
  98.0 1.8 constant_dynamic-update-slice_fusion.3
  99.9 4.0 %constant_dynamic-update-slice_fusion.2 = bf16[768,8192]{1,0:T(8,128)(2,1)} fusion(bf16[768,8192]{1,0:T(8,128)(2,1)} %constant_dynamic-update-slice_fusion.3, bf16[192,8192]{1,0:T(8,128)(2,1)} %collective-permute-done.1, s32[]{:T(128)S(6)} %select_n.39), kind=kLoop, calls=%fused_computation.27 | loop fusion | bytes 6291460 | tf_op jit(solution)/shard_map/dynamic_update_slice | solution.py:189
  103.9 38.4 %collective-permute-done.2 = bf16[96,8192]{1,0:T(8,128)(2,1)S(1)} collective-permute-done((bf16[96,8192]{1,0:T(8,128)(2,1)S(1)}, bf16[96,8192]{1,0:T(8,128)(2,1)S(1)}, u32[]{:S(2)}, u32[]{:S(2)}) %collective-permute-start.2) | collective-permute-done | bytes 1572896 | tf_op jit(solution)/shard_map/ppermute | solution.py:179
  144.9 8.4 %convolution_convert_fusion = bf16[768,32]{0,1:T(8,128)(2,1)S(1)} fusion(bf16[768,8192]{1,0:T(8,128)(2,1)} %constant_dynamic-update-slice_fusion, bf16[8192,16]{0,1:T(8,128)(2,1)S(1)} %copy-done.1, bf16[8192,16]{0,1:T(8,128)(2,1)S(1)} %copy-done.2), kind=kOutput, calls=%fused_computation.8 | convolution fusion | flops 403726336 | bytes 13156352 | tf_op jit(solution)/shard_map/dot_general | solution.py:192
  154.2 22.3 %fusion.18.q_ref.k_ref.v_ref = f32[768,1280]{1,0:T(8,128)} fusion(bf16[768,8192]{1,0:T(8,128)(2,1)} %constant_dynamic-update-slice_fusion, bf16[8192,1280]{1,0:T(8,128)(2,1)} %all-gather.4.cloned.1.call-done), kind=kOutput, calls=%fused_computation.33 | convolution fusion | flops 16106127360 | bytes 37486592 | tf_op jit(solution)/shard_map/dot_general | solution.py:193
  176.5 29.8 %attention.1 = (bf16[768,1024]{1,0:T(8,128)(2,1)}, f32[16,1024]{1,0:T(8,128)}, f32[16,128]{1,0:T(8,128)}, f32[768,32]{1,0:T(8,128)}) custom-call(f32[768,1280]{1,0:T(8,128)} %fusion.18.q_ref.k_ref.v_ref, f32[768,1280]{1,0:T(8,128)} %fusion.18.q_ref.k_ref.v_ref, f32[768,1280]{1,0:T(8,128)} %fusion.18.q_ref.k_ref.v_ref, bf16[768,32]{1,0:T(8,128)(2,1)} %copy.25.down_ref, ...), custom_call_target="tpu_custom_call" | custom-call | tf_op jit(solution)/shard_map/attention/pallas_call | solution.py:123
  208.2 3.5 %all-to-all-start.2 = ((f32[4,768,32]{1,2,0:T(8,128)}), f32[4,768,32]{1,2,0:T(8,128)S(1)}, u32[]{:S(2)}, u32[]{:S(2)}) async-start(f32[4,768,32]{1,2,0:T(8,128)} %broadcast_in_dim.8), calls=%async_computation.2 | async-start | bytes 786432 | tf_op jit(solution)/shard_map/all_to_all | solution.py:201
  213.3 5.9 %all-to-all-done.2 = f32[4,768,32]{1,2,0:T(8,128)S(1)} async-done(((f32[4,768,32]{1,2,0:T(8,128)}), f32[4,768,32]{1,2,0:T(8,128)S(1)}, u32[]{:S(2)}, u32[]{:S(2)}) %all-to-all-start.2) | async-done | bytes 393248 | tf_op jit(solution)/shard_map/all_to_all | solution.py:201
  219.3 2.5 fusion.5
  221.9 17.9 %all_to_all.45 = f32[32,8,384]{2,1,0:T(8,128)S(1)} all-to-all(f32[32,8,384]{2,1,0:T(8,128)S(1)} %bitcast.22), channel_id=1, replica_groups=mesh['dp'=4,'fsdp'=8,'tensor'=4] {'dp','fsdp'}, dimensions={0} | all-to-all | bytes 786432 | tf_op jit(solution)/shard_map/all_to_all | solution.py:218
  239.8 64.8 %all-gather = f32[256,384]{1,0:T(8,128)S(1)} all-gather(f32[8,384]{1,0:T(8,128)S(1)} %reduce_sum.29), channel_id=2, replica_groups=mesh['dp'=4,'fsdp'=8,'tensor'=4] {'dp','fsdp'}, dimensions={0}, use_global_device_ids=true | all-gather | bytes 405504 | tf_op jit(solution)/shard_map/all_gather | solution.py:219
  305.4 3.6 %all-to-all-start.1 = ((bf16[4,192,1024]{2,1,0:T(8,128)(2,1)}), bf16[4,192,1024]{2,1,0:T(8,128)(2,1)S(1)}, u32[]{:S(2)}, u32[]{:S(2)}) async-start(bf16[4,192,1024]{2,1,0:T(8,128)(2,1)} %bitcast.4), calls=%async_computation.1 | async-start | bytes 3145728 | tf_op jit(solution)/shard_map/all_to_all | solution.py:198
  310.3 20.6 %all-to-all-done.1 = bf16[4,192,1024]{2,1,0:T(8,128)(2,1)S(1)} async-done(((bf16[4,192,1024]{2,1,0:T(8,128)(2,1)}), bf16[4,192,1024]{2,1,0:T(8,128)(2,1)S(1)}, u32[]{:S(2)}, u32[]{:S(2)}) %all-to-all-start.1) | async-done | bytes 1572896 | tf_op jit(solution)/shard_map/all_to_all | solution.py:198
  332.2 2.4 broadcast_in_dim.7
  334.6 2.2 slice_bitcast_fusion
  (43 shorter events, 17.7 us)
Async XLA Ops:
  7.2 147.0 %all-gather.4.cloned.1.call-start = ((), (), s32[]{:S(2)}) async-start(), calls=%async_computation.4 | async-start | bytes 21626880 | tf_op jit(solution)/shard_map/all_gather | solution.py:171
  10.5 6.1 %copy-start = (bf16[1,192,8192]{2,1,0:T(8,128)(2,1)S(1)}, bf16[1,192,8192]{2,1,0:T(8,128)(2,1)}, u32[]{:S(2)}) copy-start(bf16[1,192,8192]{2,1,0:T(8,128)(2,1)} %param.8) | copy-start | bytes 9437188
  10.5 6.1 %copy-start.3 = (f32[8192]{0:T(1024)S(1)}, f32[8192]{0:T(1024)}, u32[]{:S(2)}) copy-start(f32[8192]{0:T(1024)} %param.9) | copy-start | bytes 98308
  20.4 72.4 %collective-permute-start = (bf16[192,8192]{1,0:T(8,128)(2,1)}, bf16[192,8192]{1,0:T(8,128)(2,1)S(1)}, u32[]{:S(2)}, u32[]{:S(2)}) collective-permute-start(bf16[192,8192]{1,0:T(8,128)(2,1)} %get-tuple-element.14), channel_id=1, source_target_pairs={{0,1},{1,2},{2,3},{3,0},{4,5},{5,6},{6,7},{7,4},{8,9},{9,10},{10,1... | collective-permute-start | bytes 9437192 | tf_op jit(solution)/shard_map/ppermute | solution.py:176
  22.1 71.4 %collective-permute-start.1 = (bf16[192,8192]{1,0:T(8,128)(2,1)}, bf16[192,8192]{1,0:T(8,128)(2,1)}, u32[]{:S(2)}, u32[]{:S(2)}) collective-permute-start(bf16[192,8192]{1,0:T(8,128)(2,1)} %get-tuple-element.14), channel_id=1, source_target_pairs={{0,3},{1,0},{2,1},{3,2},{4,7},{5,4},{6,5},{7,6},{8,11},{9,8},{10,9... | collective-permute-start | bytes 9437192 | tf_op jit(solution)/shard_map/ppermute | solution.py:177
  30.6 145.9 %all-to-all-start = ((bf16[192,4,1024]{2,0,1:T(8,128)(2,1)}), bf16[192,4,1024]{2,0,1:T(8,128)(2,1)}, u32[]{:S(2)}, u32[]{:S(2)}) async-start(bf16[192,4,1024]{2,0,1:T(8,128)(2,1)} %copy.24), calls=%async_computation | async-start | bytes 3145728 | tf_op jit(solution)/shard_map/all_to_all | solution.py:172
  92.9 49.4 %collective-permute-start.2 = (bf16[96,8192]{1,0:T(8,128)(2,1)S(1)}, bf16[96,8192]{1,0:T(8,128)(2,1)S(1)}, u32[]{:S(2)}, u32[]{:S(2)}) collective-permute-start(bf16[96,8192]{1,0:T(8,128)(2,1)S(1)} %slice.28), channel_id=1, source_target_pairs={{0,1},{1,2},{2,3},{3,0},{4,5},{5,6},{6,7},{7,4},{8,9},{9,10},{10,1... | collective-permute-start | bytes 4718600 | tf_op jit(solution)/shard_map/ppermute | solution.py:179
  95.0 48.6 %collective-permute-start.3 = (bf16[96,8192]{1,0:T(8,128)(2,1)S(1)}, bf16[96,8192]{1,0:T(8,128)(2,1)S(1)}, u32[]{:S(2)}, u32[]{:S(2)}) collective-permute-start(bf16[96,8192]{1,0:T(8,128)(2,1)S(1)} %slice.29), channel_id=1, source_target_pairs={{0,3},{1,0},{2,1},{3,2},{4,7},{5,4},{6,5},{7,6},{8,11},{9,8},{10,9... | collective-permute-start | bytes 4718600 | tf_op jit(solution)/shard_map/ppermute | solution.py:180
  99.9 45.1 %copy-start.1 = (bf16[8192,16]{0,1:T(8,128)(2,1)S(1)}, bf16[8192,16]{0,1:T(8,128)(2,1)}, u32[]{:S(2)}) copy-start(bf16[8192,16]{0,1:T(8,128)(2,1)} %param.13) | copy-start | bytes 786436
  99.9 45.1 %copy-start.2 = (bf16[8192,16]{0,1:T(8,128)(2,1)S(1)}, bf16[8192,16]{0,1:T(8,128)(2,1)}, u32[]{:S(2)}) copy-start(bf16[8192,16]{0,1:T(8,128)(2,1)} %param.11) | copy-start | bytes 786436
  208.2 11.0 %all-to-all-start.2 = ((f32[4,768,32]{1,2,0:T(8,128)}), f32[4,768,32]{1,2,0:T(8,128)S(1)}, u32[]{:S(2)}, u32[]{:S(2)}) async-start(f32[4,768,32]{1,2,0:T(8,128)} %broadcast_in_dim.8), calls=%async_computation.2 | async-start | bytes 786432 | tf_op jit(solution)/shard_map/all_to_all | solution.py:201
  211.7 122.9 %all-gather.6.cloned.1.call-start = ((), (), s32[]{:S(2)}) async-start(), calls=%async_computation.5 | async-start | bytes 1310720 | tf_op jit(solution)/shard_map/all_gather | solution.py:224
  305.4 25.6 %all-to-all-start.1 = ((bf16[4,192,1024]{2,1,0:T(8,128)(2,1)}), bf16[4,192,1024]{2,1,0:T(8,128)(2,1)S(1)}, u32[]{:S(2)}, u32[]{:S(2)}) async-start(bf16[4,192,1024]{2,1,0:T(8,128)(2,1)} %bitcast.4), calls=%async_computation.1 | async-start | bytes 3145728 | tf_op jit(solution)/shard_map/all_to_all | solution.py:198
Sparse Core Ops, SparseCore 0:
  9.6 123.8 all-gather.3
  305.5 21.5 all-gather.5
